TPU v7x, 32 devices: a whole 2x2x4 slice. The times are simulated.
32 devices in a mesh: groups: 2 (over x), rows: 16 (over z, y, core).
Axes of the slice: x: 2, y: 2, z: 4, core: 2. Of those that a mesh axis runs over, the one named last changes fastest.
Arguments:
- queries: bfloat16 [2048, 8192], P(('groups', 'rows')), parts along dimension 0, may hold values from -6 to 6
- sketches: bfloat16 [16384, 8192], P(('groups', 'rows')), parts along dimension 0, may hold values from -16 to 16, as said below
- row_ids: int32 [16384], P(('groups', 'rows')), parts along dimension 0, may hold values from 0 to 8191, each once
Outputs:
- top_scores: float32 [2048, 128], P(('groups', 'rows')), parts along dimension 0
There are 2 independent parts, one for each index of `groups`. A program takes and returns all parts, laid end to end along the dimension named above; each array names one. Nothing has to cross between parts.
Inputs may be any that keep to these rules, and one draw needn't show every extreme that they name: `sketches`: sketch entries are real-valued.
All inputs are finite; a program needn't handle non-finite values.
Results may differ from a plain program's by a relative error of at most 0.0003.
Values may be sent and summed in bfloat16 or wider, within the bound.
A program may use at most 128 MiB of HBM per device.

v0:
```python
import jax
import jax.numpy as jnp
from jax import lax
from jax.sharding import PartitionSpec as P

TOPK = 128


def shards(queries, sketches, row_ids):
    devices = lax.axis_size("rows")
    total_rows = sketches.shape[0] * devices
    retired = total_rows // 4
    live_count = total_rows - retired
    keep = TOPK
    scores = lax.dot_general(
        lax.all_gather(queries, "rows", axis=0, tiled=True),
        sketches,
        (((1,), (1,)), ((), ())),
        preferred_element_type=jnp.float32,
    )
    live = row_ids >= retired
    square_sum = jnp.sum(jnp.where(live[None, :], scores * scores, jnp.float32(0.0)), axis=1)
    masked = jnp.where(live[None, :], scores, jnp.float32(-1e30))
    candidates = lax.top_k(masked, keep)[0]
    payload = (candidates, square_sum[:, None])
    received = (
        lax.all_to_all(payload[0], "rows", split_axis=0, concat_axis=1, tiled=True),
        lax.all_to_all(payload[1], "rows", split_axis=0, concat_axis=1, tiled=True),
    )
    best = lax.top_k(received[0], keep)[0]
    own_sum = jnp.sum(received[1], axis=1)
    inverse_scale = lax.rsqrt(own_sum / jnp.float32(live_count) + jnp.float32(1e-06))
    return best * inverse_scale[:, None]


def solution(mesh):
    return jax.shard_map(
        shards,
        mesh=mesh,
        in_specs=(P(("groups", "rows"), None), P(("groups", "rows"), None), P(("groups", "rows"))),
        out_specs=P(("groups", "rows"), None),
        check_vma=False,
    )
```

profile of v0, /device:TPU:0, one launch (start us, length us, event | category | flops | bytes accessed | tf_op | source)
XLA Modules:
  0.0 261.9 jit_solution(8203778866880331875)
XLA Ops:
  6.5 0.0 all-gather.2.cloned.1.call-start
  6.5 0.7 all-gather.2.cloned.1.call-update
  7.3 0.7 broadcast_compare_fusion
  7.9 130.7 %all-gather.2.cloned.1.call-done = bf16[1024,8192]{1,0:T(8,128)(2,1)} async-done(((bf16[64,8192]{1,0:T(8,128)(2,1)}), bf16[1024,8192]{1,0:T(8,128)(2,1)}) %all-gather.2.cloned.1.call-update) | async-done | bytes 16777232 | tf_op jit(solution)/shard_map/all_gather | solution.py:16
  138.7 15.9 %select_reduce_fusion = (f32[1024]{0:T(1024)S(1)}, f32[1024,512]{0,1:T(8,128)}) fusion(pred[512]{0:T(512)(128)(4,1)S(1)} %broadcast_compare_fusion, bf16[1024,8192]{1,0:T(8,128)(2,1)} %all-gather.2.cloned.1.call-done, bf16[512,8192]{1,0:T(8,128)(2,1)} %param.4), kind=kOutput, calls=%fused_computation | convolution fusion | flops 8592030720 | bytes 27267584 | tf_op jit(solution)/shard_map/dot_general | solution.py:15
  154.5 0.7 all_to_all.28
  155.2 3.5 %all-to-all-start.1 = ((f32[16,64,1]{1,2,0:T(1,128)}), f32[16,64,1]{1,2,0:T(1,128)S(1)}, u32[]{:S(2)}, u32[]{:S(2)}) async-start(f32[16,64,1]{1,2,0:T(1,128)} %bitcast.2), calls=%async_computation.1 | async-start | bytes 16384 | tf_op jit(solution)/shard_map/all_to_all | solution.py:28
  158.7 0.1 iota.6.clone
  158.8 58.5 %top_k.14 = (f32[1024,512]{0,1:T(8,128)}, s32[1024,512]{0,1:T(8,128)}) sort(f32[1024,512]{0,1:T(8,128)} %get-tuple-element.15, s32[1024,512]{0,1:T(8,128)S(1)} %iota.6.clone), dimensions={1}, to_apply=%region_0.1 | sort | flops 9961472 | bytes 8388608 | tf_op jit(solution)/shard_map/top_k | solution.py:24
  217.3 1.9 copy.11
  219.3 0.9 top_k.22
  220.1 0.0 all-to-all-done.1
  220.1 6.0 %all-to-all-start = ((f32[16,64,128]{2,1,0:T(8,128)}), f32[16,64,128]{2,1,0:T(8,128)S(1)}, u32[]{:S(2)}, u32[]{:S(2)}) async-start(f32[16,64,128]{2,1,0:T(8,128)} %bitcast), calls=%async_computation | async-start | bytes 1048576 | tf_op jit(solution)/shard_map/all_to_all | solution.py:27
  226.2 14.2 %all-to-all-done = f32[16,64,128]{2,1,0:T(8,128)S(1)} async-done(((f32[16,64,128]{2,1,0:T(8,128)}), f32[16,64,128]{2,1,0:T(8,128)S(1)}, u32[]{:S(2)}, u32[]{:S(2)}) %all-to-all-start) | async-done | bytes 524320 | tf_op jit(solution)/shard_map/all_to_all | solution.py:27
  240.4 14.0 %sort_prefixfusion = f32[64,128]{1,0:T(8,128)S(1)} fusion(f32[64,2048]{1,0:T(8,128)S(1)} %copy_bitcast_fusion), kind=kCustom, calls=%top_k.20.sort_prefix | custom fusion | flops 2228224 | bytes 557056 | tf_op jit(solution)/shard_map/top_k | solution.py:30
  254.4 0.7 broadcast_multiply_fusion
  (3 shorter events, 0.1 us)
Async XLA Ops:
  6.5 132.1 %all-gather.2.cloned.1.call-start = ((), (), s32[]{:S(2)}) async-start(), calls=%async_computation.2 | async-start | bytes 17825792 | tf_op jit(solution)/shard_map/all_gather | solution.py:16
  155.2 64.9 %all-to-all-start.1 = ((f32[16,64,1]{1,2,0:T(1,128)}), f32[16,64,1]{1,2,0:T(1,128)S(1)}, u32[]{:S(2)}, u32[]{:S(2)}) async-start(f32[16,64,1]{1,2,0:T(1,128)} %bitcast.2), calls=%async_computation.1 | async-start | bytes 16384 | tf_op jit(solution)/shard_map/all_to_all | solution.py:28
  220.1 20.2 %all-to-all-start = ((f32[16,64,128]{2,1,0:T(8,128)}), f32[16,64,128]{2,1,0:T(8,128)S(1)}, u32[]{:S(2)}, u32[]{:S(2)}) async-start(f32[16,64,128]{2,1,0:T(8,128)} %bitcast), calls=%async_computation | async-start | bytes 1048576 | tf_op jit(solution)/shard_map/all_to_all | solution.py:27
Sparse Core Ops, SparseCore 0:
  9.5 129.1 all-gather.1
where the time goes:
time: 262 us
  waiting for transfers between devices  146 us (56%)
  other arithmetic  73.9 us (28%)
  matrix products  15.9 us (6%)
  between operations  13.4 us (5%)
  starting transfers between devices  9.45 us (4%)
  local copies, waits for them, and re-layouts  3.62 us (1%)
    all_gather x1, waiting for transfers between devices, shards(): lax.all_gather(queries, 'rows', axis=0, tiled=True)  131 us
    top_k x1, other arithmetic, shards(): candidates = lax.top_k(masked, keep)[0]  58.5 us
    dot_general x1, matrix products, shards(): lax.dot_general(lax.all_gather(queries, 'rows', axis=0, tiled=True), sket...  15.9 us
    all_to_all x1, waiting for transfers between devices, shards(): lax.all_to_all(payload[0], 'rows', split_axis=0, concat_axis=1, tiled=True)  14.2 us
    top_k x1, other arithmetic, shards(): best = lax.top_k(received[0], keep)[0]  14 us
    all_to_all x1, starting transfers between devices, shards(): lax.all_to_all(payload[0], 'rows', split_axis=0, concat_axis=1, tiled=True)  5.98 us
  transfers between devices with their start and end apart: 3, of which 2 were waited for; matrix products, arithmetic and copies ran while one was open for 24% of the time, Pallas kernels for 0%

commit v1 on v0

v1 whole, which is shorter than its diff:
```python
import functools

import jax
import jax.numpy as jnp
from jax import lax
from jax.experimental import pallas as pl
from jax.experimental.pallas import tpu as pltpu
from jax.sharding import PartitionSpec as P

TOPK = 128
LANES = 128
SUBLANES = 8
SPLIT = 4
NEG = -1e30
MESH = pl.DeviceIdType.MESH


def exchange(x, low, high, dist):
    n = x.shape[0]
    mid = x[low:high].reshape((high - low) // (2 * dist), 2, dist, SUBLANES, LANES)
    a, b = mid[:, 0], mid[:, 1]
    mid = jnp.concatenate([jnp.maximum(a, b)[:, None], jnp.minimum(a, b)[:, None]], axis=1)
    mid = mid.reshape(high - low, SUBLANES, LANES)
    parts = ([x[:low]] if low else []) + [mid] + ([x[high:]] if high < n else [])
    return jnp.concatenate(parts, axis=0) if len(parts) > 1 else mid


def sort_rows(x):
    n = x.shape[0]
    p = 1
    while p < n:
        x = exchange(x, 0, n, p)
        k = p // 2
        while k >= 1:
            blocks = x.reshape(n // (2 * p), 2 * p, SUBLANES, LANES)
            mid = blocks[:, k : 2 * p - k]
            count = (2 * p - 2 * k) // (2 * k)
            mid = mid.reshape(n // (2 * p), count, 2, k, SUBLANES, LANES)
            a, b = mid[:, :, 0], mid[:, :, 1]
            mid = jnp.concatenate([jnp.maximum(a, b)[:, :, None], jnp.minimum(a, b)[:, :, None]], axis=2)
            mid = mid.reshape(n // (2 * p), 2 * p - 2 * k, SUBLANES, LANES)
            x = jnp.concatenate([blocks[:, :k], mid, blocks[:, 2 * p - k :]], axis=1).reshape(n, SUBLANES, LANES)
            k //= 2
        p *= 2
    return x


def reverse_rows(x):
    n = x.shape[0]
    d = n // 2
    while d >= 1:
        y = x.reshape(n // (2 * d), 2, d, SUBLANES, LANES)
        x = jnp.concatenate([y[:, 1:], y[:, :1]], axis=1).reshape(n, SUBLANES, LANES)
        d //= 2
    return x


def merge_rolled(x, shift, axis):
    n = x.shape[0]
    size = x.shape[axis]
    rolled = pltpu.roll(x, size - shift, axis)
    x = jnp.maximum(x, reverse_rows(rolled))
    d = n // 2
    while d >= 1:
        x = exchange(x, 0, n, d)
        d //= 2
    return x


def compact(x):
    n = x.shape[0]
    y = x.reshape(n // SUBLANES, SUBLANES, SUBLANES, LANES)
    sub = lax.broadcasted_iota(jnp.int32, (n // SUBLANES, SUBLANES, LANES), 1)
    out = y[:, 0]
    for s in range(1, SUBLANES):
        out = jnp.where(sub == s, y[:, s], out)
    return out.reshape(n, LANES)


def kernel(n, retired, live_count, q_in, sk_in, id_in, out, qb, sk, idb, acc, sendb, recvb, tb,
           q_send, q_recv, c_send, c_recv, s_load, s_send, s_recv, own_sem, id_sem):
    nq, width = q_in.shape
    rows = sk_in.shape[0]
    wk = width // SPLIT
    per = LANES // nq
    groups = n // per
    steps = per // 2
    last = n // 2 - 1
    device = lax.axis_index("rows")
    core = device % 2
    chip = device // 2
    pos = chip // 2 + (chip % 2) * (n - 1 - 2 * (chip // 2))

    def at(position):
        p = (position + n) % n
        h = p // (n // 2)
        c = (1 - h) * (2 * p) + h * (2 * (n - 1 - p) + 1)
        return {"rows": c * 2 + core}

    right, left = at(pos + 1), at(pos - 1)
    partner = {"rows": chip * 2 + 1 - core}
    own = n - 1

    def slot_rows(slot):
        return pl.ds(pl.multiple_of(slot * nq, nq), nq)

    loads = []
    for s in range(SPLIT):
        loads.append(pltpu.make_async_copy(q_in.at[:, pl.ds(s * wk, wk)], qb.at[s, slot_rows(own)], own_sem.at[s]))
    for copy in loads:
        copy.start()
    sk_loads = []
    for s in range(SPLIT):
        sk_loads.append(pltpu.make_async_copy(sk_in.at[:, pl.ds(s * wk, wk)], sk.at[s, pl.ds(0, rows)], s_load.at[s]))
    for copy in sk_loads:
        copy.start()

    barrier = pltpu.get_barrier_semaphore()
    for j in range(1, n):
        pl.semaphore_signal(barrier, inc=1, device_id=at(pos + j), device_id_type=MESH)
    pl.semaphore_signal(barrier, inc=1, device_id=partner, device_id_type=MESH)
    pl.semaphore_wait(barrier, n)

    def q_copy(s, src, dst, target):
        return pltpu.make_async_remote_copy(
            src_ref=qb.at[s, slot_rows(src)], dst_ref=qb.at[s, slot_rows(dst)],
            send_sem=q_send.at[s, dst], recv_sem=q_recv.at[s, dst],
            device_id=target, device_id_type=MESH)

    for s in range(SPLIT):
        loads[s].wait()
        q_copy(s, own, 0, right).start()
        q_copy(s, own, 1, left).start()
    sk_sends = []
    for s in range(SPLIT):
        sk_sends.append(pltpu.make_async_remote_copy(
            src_ref=sk_in.at[:, pl.ds(s * wk, wk)], dst_ref=sk.at[s, pl.ds(rows, rows)],
            send_sem=s_send.at[s], recv_sem=s_recv.at[s], device_id=partner, device_id_type=MESH))
    id_send = pltpu.make_async_remote_copy(
        src_ref=id_in, dst_ref=idb.at[pl.ds(rows, rows)], send_sem=id_sem.at[0], recv_sem=id_sem.at[1],
        device_id=partner, device_id_type=MESH)
    for copy in sk_sends:
        copy.start()
    id_send.start()
    idb[pl.ds(0, rows)] = id_in[...]
    for copy in sk_loads:
        copy.wait()
    for copy in sk_sends:
        copy.wait()
    id_send.wait()

    def arrive(t, s):
        q_copy(s, 2 * t - 2, 2 * t - 2, right).wait_recv()
        q_copy(s, 2 * t - 1, 2 * t - 1, left).wait_recv()

        @pl.when(t < last)
        def _():
            q_copy(s, 2 * t - 2, 2 * t, right).start()
            q_copy(s, 2 * t - 1, 2 * t + 1, left).start()

        @pl.when((t == last) & (s < SPLIT // 2))
        def _():
            q_copy(s, 2 * t - 2, n - 2, right).start()

        @pl.when((t == last) & (s >= SPLIT // 2))
        def _():
            q_copy(s, 2 * t - 1, n - 2, left).start()

    def multiply(g, s):
        q = qb[s, pl.ds(pl.multiple_of(g * LANES, LANES), LANES)]
        acc[...] += lax.dot_general(sk[s], q, (((1,), (1,)), ((), ())), preferred_element_type=jnp.float32)

    def c_copy(slot, target):
        return pltpu.make_async_remote_copy(
            src_ref=sendb.at[slot], dst_ref=recvb.at[slot],
            send_sem=c_send.at[slot], recv_sem=c_recv.at[slot], device_id=target, device_id_type=MESH)

    def select(g, store_own):
        live = idb[...] >= retired
        scores = acc[...]
        square = jnp.where(live, scores * scores, 0.0).reshape(2 * rows // SUBLANES, SUBLANES, LANES).sum(axis=0)
        x = jnp.where(live, scores, NEG).reshape(2 * rows // SUBLANES, SUBLANES, LANES)
        x = sort_rows(x)
        shift = SUBLANES // 2
        while shift >= 1:
            x = merge_rolled(x, shift, 1)
            shift //= 2
        y = compact(x).T
        for p in range(per):
            slot = g * per + p
            target = recvb if store_own and p == per - 1 else sendb
            target[slot, pl.ds(0, nq)] = y[p * nq : (p + 1) * nq]
            target[slot, pl.ds(nq, SUBLANES)] = square
        for p in range(per - 1 if store_own else per):
            slot = g * per + p
            t = slot // 2 + 1
            c_copy(slot, at(pos - t) if p % 2 == 0 else at(pos + t)).start()

    def group(g, carry):
        acc[...] = jnp.zeros_like(acc)

        @pl.loop(0, steps)
        def _(u):
            @pl.loop(0, SPLIT)
            def _(s):
                arrive(g * steps + u + 1, s)
                if steps == 1:
                    multiply(g, s)

        if steps > 1:
            @pl.loop(0, SPLIT)
            def _(s):
                multiply(g, s)

        select(g, False)
        return carry

    lax.fori_loop(0, groups - 1, group, 0)

    acc[...] = jnp.zeros_like(acc)
    if steps > 1:
        @pl.loop(0, steps - 1)
        def _(u):
            @pl.loop(0, SPLIT)
            def _(s):
                arrive((groups - 1) * steps + u + 1, s)

    @pl.loop(0, SPLIT // 2)
    def _(h):
        for s in (h, h + SPLIT // 2):
            q_copy(s, n - 2, n - 2, right).wait_recv()
            multiply(groups - 1, s)

    select(groups - 1, True)

    @pl.loop(0, n - 2)
    def _(slot):
        @pl.loop(0, SPLIT)
        def _(s):
            q_copy(s, slot, slot, right).wait_send()

    @pl.loop(0, SPLIT)
    def _(s):
        q_copy(s, n - 2, n - 2, right).wait_send()

    @pl.loop(0, n - 1)
    def _(slot):
        c_copy(slot, right).wait()

    square = jnp.zeros((SUBLANES, LANES), jnp.float32)
    for p in range(per):
        part = recvb[p, pl.ds(nq, SUBLANES)]
        for g in range(1, groups):
            part += recvb[g * per + p, pl.ds(nq, SUBLANES)]
        square += pltpu.roll(part, (LANES - p * nq) % LANES, 1) if p else part
    total = jnp.sum(square, axis=0, keepdims=True)
    scale = lax.rsqrt(total / jnp.float32(live_count) + jnp.float32(1e-06))

    for g in range(groups):
        y = jnp.concatenate([recvb[g * per + p, pl.ds(0, nq)] for p in range(per)], axis=0).T
        for copy in range(SUBLANES // groups):
            tb[pl.ds((copy * groups + g) * TOPK, TOPK)] = y
    x = jnp.concatenate([tb[pl.ds(i, SUBLANES, TOPK)][None] for i in range(TOPK)], axis=0)
    shift = groups // 2
    while shift >= 1:
        x = merge_rolled(x, shift, 1)
        shift //= 2
    shift = LANES // 2
    while shift >= nq:
        x = merge_rolled(x, shift, 2)
        shift //= 2
    out[...] = (compact(x) * scale).T[:nq]


def shards(queries, sketches, row_ids):
    devices = lax.axis_size("rows")
    total_rows = sketches.shape[0] * devices
    retired = total_rows // 4
    live_count = total_rows - retired
    n = devices // 2
    nq, width = queries.shape
    rows = sketches.shape[0]
    wk = width // SPLIT
    ids = jnp.broadcast_to(row_ids[:, None], (rows, LANES))
    vmem = pl.BlockSpec(memory_space=pltpu.VMEM)
    hbm = pl.BlockSpec(memory_space=pl.ANY)
    return pl.pallas_call(
        functools.partial(kernel, n, retired, live_count),
        out_shape=jax.ShapeDtypeStruct((nq, TOPK), jnp.float32),
        in_specs=[hbm, hbm, vmem],
        out_specs=vmem,
        scratch_shapes=[
            pltpu.VMEM((SPLIT, n * nq, wk), jnp.bfloat16),
            pltpu.VMEM((SPLIT, 2 * rows, wk), jnp.bfloat16),
            pltpu.VMEM((2 * rows, LANES), jnp.int32),
            pltpu.VMEM((2 * rows, LANES), jnp.float32),
            pltpu.VMEM((n, nq + SUBLANES, TOPK), jnp.float32),
            pltpu.VMEM((n, nq + SUBLANES, TOPK), jnp.float32),
            pltpu.VMEM((SUBLANES * TOPK, LANES), jnp.float32),
            pltpu.SemaphoreType.DMA((SPLIT, n)),
            pltpu.SemaphoreType.DMA((SPLIT, n)),
            pltpu.SemaphoreType.DMA((n,)),
            pltpu.SemaphoreType.DMA((n,)),
            pltpu.SemaphoreType.DMA((SPLIT,)),
            pltpu.SemaphoreType.DMA((SPLIT,)),
            pltpu.SemaphoreType.DMA((SPLIT,)),
            pltpu.SemaphoreType.DMA((SPLIT,)),
            pltpu.SemaphoreType.DMA((2,)),
        ],
        compiler_params=pltpu.CompilerParams(
            collective_id=0, has_side_effects=True, vmem_limit_bytes=60 * 1024 * 1024
        ),
        name="attribution",
    )(queries, sketches, ids)


def solution(mesh):
    return jax.shard_map(
        shards,
        mesh=mesh,
        in_specs=(P(("groups", "rows"), None), P(("groups", "rows"), None), P(("groups", "rows"))),
        out_specs=P(("groups", "rows"), None),
        check_vma=False,
    )
```

time: 262 us -> 104 us (0.40)
  waiting for transfers between devices: 146 us -> 0 us
  Pallas kernels: 0 us -> 101 us
  other arithmetic: 73.9 us -> 0 us
  matrix products: 15.9 us -> 0 us
  between operations: 13.4 us -> 0.01 us
  starting transfers between devices: 9.45 us -> 0 us
    all_gather x1 -> x0, waiting for transfers between devices: 131 us -> none  [shards(): lax.all_gather(queries, 'rows', axis=0, tiled=True)]
    pallas_call x0 -> x1, Pallas kernels: none -> 101 us  [shards(): pl.pallas_call(functools.partial(kernel, n, retired, live_count), out_sha...]
    top_k x2 -> x0, other arithmetic: 72.5 us -> none  [the longest x1 58.5 us: shards(): candidates = lax.top_k(masked, keep)[0]]
    dot_general x1 -> x0, matrix products: 15.9 us -> none  [shards(): lax.dot_general(lax.all_gather(queries, 'rows', axis=0, tiled=True), sket...]
    all_to_all x2 -> x0, waiting for transfers between devices: 14.2 us -> none  [the longest x1 14.2 us: shards(): lax.all_to_all(payload[0], 'rows', split_axis=0, concat_axis=1, tiled=True)]
    all_to_all x2 -> x0, starting transfers between devices: 9.45 us -> none  [the longest x1 5.98 us: shards(): lax.all_to_all(payload[0], 'rows', split_axis=0, concat_axis=1, tiled=True)]
    top_k x2 -> x0, local copies, waits for them, and re-layouts: 2.78 us -> none  [shards(): candidates = lax.top_k(masked, keep)[0]]
  transfers between devices with their start and end apart: 3 -> 0, of which waited for: 2 -> 0; matrix products, arithmetic and copies ran while one was open for 24% -> 0% of each run, Pallas kernels for 0% -> 0%
where the time goes in v1:
time: 104 us
  Pallas kernels  101 us (97%)
  local copies, waits for them, and re-layouts  2.88 us (3%)
    pallas_call x1, Pallas kernels, shards(): pl.pallas_call(functools.partial(kernel, n, retired, live_count), out_sha...  101 us

profile of v1, /device:TPU:0, one launch (start us, length us, event | category | flops | bytes accessed | tf_op | source)
XLA Modules:
  0.0 104.0 jit_solution(11956407682296112306)
XLA Ops:
  0.0 1.5 %broadcast_in_dim.2.id_in = s32[512,128]{1,0:T(8,128)} broadcast(s32[512]{0:T(512)} %param.5), dimensions={0} | broadcast | bytes 264192 | tf_op jit(solution)/shard_map/broadcast_in_dim | solution.py:284
  1.5 101.1 %attribution.1 = f32[64,128]{1,0:T(8,128)} custom-call(bf16[64,8192]{1,0:T(8,128)(2,1)} %q_in.1, bf16[512,8192]{1,0:T(8,128)(2,1)} %sk_in.1, s32[512,128]{1,0:T(8,128)} %broadcast_in_dim.2.id_in), custom_call_target="tpu_custom_call" | custom-call | tf_op jit(solution)/shard_map/attribution/pallas_call | solution.py:287
  102.6 1.4 %copy.5 = f32[64,128]{1,0:T(8,128)} copy(f32[64,128]{1,0:T(8,128)} %attribution.1) | data formatting | bytes 65536

commit v2 on v1

--- a/solution.py
+++ b/solution.py
@@ -10,7 +10,7 @@
 TOPK = 128
 LANES = 128
 SUBLANES = 8
-SPLIT = 4
+SPLIT = 8
 NEG = -1e30
 MESH = pl.DeviceIdType.MESH
 
@@ -78,7 +78,7 @@
 
 
 def kernel(n, retired, live_count, q_in, sk_in, id_in, out, qb, sk, idb, acc, sendb, recvb, tb,
-           q_send, q_recv, c_send, c_recv, s_load, s_send, s_recv, own_sem, id_sem):
+           q_send, q_recv, c_send, c_recv, s_load, s_send, s_recv, own_sem, id_sem, id_load_sem):
     nq, width = q_in.shape
     rows = sk_in.shape[0]
     wk = width // SPLIT
@@ -114,6 +114,8 @@
         sk_loads.append(pltpu.make_async_copy(sk_in.at[:, pl.ds(s * wk, wk)], sk.at[s, pl.ds(0, rows)], s_load.at[s]))
     for copy in sk_loads:
         copy.start()
+    id_load = pltpu.make_async_copy(id_in, idb.at[pl.ds(0, rows)], id_load_sem.at[0])
+    id_load.start()
 
     barrier = pltpu.get_barrier_semaphore()
     for j in range(1, n):
@@ -142,7 +144,7 @@
     for copy in sk_sends:
         copy.start()
     id_send.start()
-    idb[pl.ds(0, rows)] = id_in[...]
+    id_load.wait()
     for copy in sk_loads:
         copy.wait()
     for copy in sk_sends:
@@ -243,21 +245,15 @@
     def _(s):
         q_copy(s, n - 2, n - 2, right).wait_send()
 
-    @pl.loop(0, n - 1)
+    @pl.loop(0, n - 2)
     def _(slot):
         c_copy(slot, right).wait()
 
-    square = jnp.zeros((SUBLANES, LANES), jnp.float32)
-    for p in range(per):
-        part = recvb[p, pl.ds(nq, SUBLANES)]
-        for g in range(1, groups):
-            part += recvb[g * per + p, pl.ds(nq, SUBLANES)]
-        square += pltpu.roll(part, (LANES - p * nq) % LANES, 1) if p else part
-    total = jnp.sum(square, axis=0, keepdims=True)
-    scale = lax.rsqrt(total / jnp.float32(live_count) + jnp.float32(1e-06))
-
     for g in range(groups):
-        y = jnp.concatenate([recvb[g * per + p, pl.ds(0, nq)] for p in range(per)], axis=0).T
+        parts = [recvb[g * per + p, pl.ds(0, nq)] for p in range(per)]
+        if g == groups - 1:
+            parts[per - 2] = jnp.full((nq, TOPK), NEG, jnp.float32)
+        y = jnp.concatenate(parts, axis=0).T
         for copy in range(SUBLANES // groups):
             tb[pl.ds((copy * groups + g) * TOPK, TOPK)] = y
     x = jnp.concatenate([tb[pl.ds(i, SUBLANES, TOPK)][None] for i in range(TOPK)], axis=0)
@@ -269,7 +265,33 @@
     while shift >= nq:
         x = merge_rolled(x, shift, 2)
         shift //= 2
-    out[...] = (compact(x) * scale).T[:nq]
+    tb[pl.ds(0, TOPK)] = compact(reverse_rows(x))
+
+    c_copy(n - 2, right).wait()
+    square = jnp.zeros((SUBLANES, LANES), jnp.float32)
+    for p in range(per):
+        part = recvb[p, pl.ds(nq, SUBLANES)]
+        for g in range(1, groups):
+            part += recvb[g * per + p, pl.ds(nq, SUBLANES)]
+        square += pltpu.roll(part, (LANES - p * nq) % LANES, 1) if p else part
+    total = jnp.sum(square, axis=0, keepdims=True)
+    scale = lax.rsqrt(total / jnp.float32(live_count) + jnp.float32(1e-06))
+
+    late = recvb[n - 2, pl.ds(0, nq)]
+    if nq < LANES:
+        late = jnp.concatenate([late, jnp.zeros((LANES - nq, TOPK), jnp.float32)], axis=0)
+    m = jnp.maximum(tb[pl.ds(0, TOPK)], late.T).reshape(TOPK // SUBLANES, SUBLANES, LANES)
+    d = TOPK // SUBLANES // 2
+    while d >= 1:
+        m = exchange(m, 0, TOPK // SUBLANES, d)
+        d //= 2
+    sub = lax.broadcasted_iota(jnp.int32, m.shape, 1)
+    d = SUBLANES // 2
+    while d >= 1:
+        after, before = pltpu.roll(m, SUBLANES - d, 1), pltpu.roll(m, d, 1)
+        m = jnp.where((sub & d) == 0, jnp.maximum(m, after), jnp.minimum(m, before))
+        d //= 2
+    out[...] = (m.reshape(TOPK, LANES) * scale).T[:nq]
 
 
 def shards(queries, sketches, row_ids):
@@ -287,7 +309,7 @@
     return pl.pallas_call(
         functools.partial(kernel, n, retired, live_count),
         out_shape=jax.ShapeDtypeStruct((nq, TOPK), jnp.float32),
-        in_specs=[hbm, hbm, vmem],
+        in_specs=[hbm, hbm, hbm],
         out_specs=vmem,
         scratch_shapes=[
             pltpu.VMEM((SPLIT, n * nq, wk), jnp.bfloat16),
@@ -306,6 +328,7 @@
             pltpu.SemaphoreType.DMA((SPLIT,)),
             pltpu.SemaphoreType.DMA((SPLIT,)),
             pltpu.SemaphoreType.DMA((2,)),
+            pltpu.SemaphoreType.DMA((1,)),
         ],
         compiler_params=pltpu.CompilerParams(
             collective_id=0, has_side_effects=True, vmem_limit_bytes=60 * 1024 * 1024

time: 104 us -> 102 us (0.981)
  Pallas kernels: 101 us -> 98.4 us
    pallas_call x1, Pallas kernels: 101 us -> 98.4 us  [shards(): pl.pallas_call(functools.partial(kernel, n, retired, live_count), out_sha...]
where the time goes in v2:
time: 102 us; the launch traced here: 101 us
  Pallas kernels  98.4 us (96%)
  local copies, waits for them, and re-layouts  2.88 us (3%)
    pallas_call x1, Pallas kernels, shards(): pl.pallas_call(functools.partial(kernel, n, retired, live_count), out_sha...  98.4 us

profile of v2, /device:TPU:0, one launch (start us, length us, event | category | flops | bytes accessed | tf_op | source)
XLA Modules:
  0.0 101.3 jit_solution(6574824998178663484)
XLA Ops:
  0.0 1.5 %broadcast_in_dim.2.id_in = s32[512,128]{1,0:T(8,128)} broadcast(s32[512]{0:T(512)} %param.5), dimensions={0} | broadcast | bytes 264192 | tf_op jit(solution)/shard_map/broadcast_in_dim | solution.py:306
  1.5 98.4 %attribution.1 = f32[64,128]{1,0:T(8,128)} custom-call(bf16[64,8192]{1,0:T(8,128)(2,1)} %q_in.1, bf16[512,8192]{1,0:T(8,128)(2,1)} %sk_in.1, s32[512,128]{1,0:T(8,128)} %broadcast_in_dim.2.id_in), custom_call_target="tpu_custom_call" | custom-call | tf_op jit(solution)/shard_map/attribution/pallas_call | solution.py:309
  99.9 1.4 %copy.5 = f32[64,128]{1,0:T(8,128)} copy(f32[64,128]{1,0:T(8,128)} %attribution.1) | data formatting | bytes 65536
